TPU v7x, 128 devices: a whole 4x4x4 slice. The times are simulated.
128 devices in a mesh: grp: 8 (over x, core), ex: 16 (over z, y).
Axes of the slice: x: 4, y: 4, z: 4, core: 2. Of those that a mesh axis runs over, the one named last changes fastest.
Arguments:
- item_ids: int32 [256, 256], P(('grp', 'ex')), may hold values from 0 to 65535, as said below
- lengths: int32 [256], P(('grp', 'ex')), may hold values from 32 to 256
- expert_ids: int32 [65536, 2], P(('grp', 'ex')), may hold values from 0 to 31, all different within a row; in each aligned block of 512 rows (0 to 511, 512 to 1023, ...) at most 48 rows name the same one
- gate_weights: float32 [65536, 2], P(('grp', 'ex')), may hold values from 0.1 to 1
- table: bfloat16 [65536, 512], P('ex'), may hold values from -6 to 6
- norm_gain: float32 [512], replicated, may hold values from 0.1 to 1.9
- w_gate: bfloat16 [32, 512, 1024], P('ex'), may hold values from -0.25 to 0.25
- w_up: bfloat16 [32, 512, 1024], P('ex'), may hold values from -0.25 to 0.25
- w_down: bfloat16 [32, 512, 1024], P('ex'), may hold values from -0.1875 to 0.1875
- d_out: bfloat16 [65536, 512], P(('grp', 'ex')), may hold values from -0.59765625 to 0.59765625
Outputs:
- layer_out: bfloat16 [65536, 512], P(('grp', 'ex'))
- grad_gate: float32 [32, 512, 1024], P('ex', None, 'grp')
- grad_up: float32 [32, 512, 1024], P('ex', None, 'grp')
- grad_down: float32 [32, 512, 1024], P('ex', None, 'grp')
Inputs may be any that keep to these rules, and one draw needn't show every extreme that they name: `item_ids`: split the ids into blocks of 4096 consecutive values. Among the 512 positions of each aligned run of 2 sequences, at most 128 name ids of one such block, and in every such run some block is named exactly 128 times. `expert_ids`: each token names 2 different experts. Within each aligned block of 512 tokens no expert is named more than 48 times, and in some block some expert is named exactly 48 times.
All inputs are finite; a program needn't handle non-finite values.
Results may differ from a plain program's by a relative error of at most 0.012.
Values may be sent and summed in bfloat16 or wider, within the bound.
No kernel may reach another device: no remote copies, remote signals or barrier semaphores. Data moves between devices by JAX's collectives and lax.ppermute only.
A program may use at most 128 MiB of HBM per device.

v0:
```python
import jax
import jax.numpy as jnp
from jax import lax
from jax.experimental import pallas as pl
from jax.experimental.pallas import tpu as pltpu
from jax.sharding import PartitionSpec as P


CAP = 48
ROW_CAP = 128
EPSILON = 1e-06
BF = jnp.bfloat16
F32 = jnp.float32
I32 = jnp.int32


def dot(a, b, dims=((1,), (0,))):
    return lax.dot_general(a, b, (dims, ((), ())), preferred_element_type=F32)


def ones_where(mask):
    return jnp.where(mask, 1.0, 0.0).astype(BF)


def shape(dims, dtype):
    return jax.ShapeDtypeStruct(dims, dtype)


def stay(*arrays):
    return [pltpu.with_memory_space_constraint(x, pltpu.HBM) for x in arrays]


def call(body, out_shape, mib, **kw):
    return pl.pallas_call(
        body,
        out_shape=out_shape,
        compiler_params=pltpu.CompilerParams(vmem_limit_bytes=mib * 1024 * 1024),
        **kw,
    )


def index_body(len_ref, ids_ref, exp_ref, gw_ref, d_ref, out_ref, rows_ref, cols_ref):
    seqs, seq_len = ids_ref.shape
    tok = seqs * seq_len
    blocks = out_ref.shape[0]
    width = d_ref.shape[1]
    routed = out_ref.shape[1] - 8
    experts = blocks * routed // CAP
    ids = jnp.concatenate([ids_ref[i : i + 1, :] for i in range(seqs)], axis=1)
    upper = ones_where(
        lax.broadcasted_iota(I32, (tok, tok), 0) < lax.broadcasted_iota(I32, (tok, tok), 1)
    )
    low = ids % 4096
    block = ids // 4096
    in_block = lax.broadcasted_iota(I32, (blocks, tok), 0) == block
    e0 = exp_ref[0:1, :]
    e1 = exp_ref[1:2, :]
    expert_iota = lax.broadcasted_iota(I32, (experts, tok), 0)
    hot0 = expert_iota == e0
    hot1 = expert_iota == e1
    cum_b = dot(ones_where(in_block), upper)
    cum_e = dot(ones_where(jnp.logical_or(hot0, hot1)), upper)
    rank_b = jnp.sum(jnp.where(in_block, cum_b, 0.0), axis=0, keepdims=True).astype(I32)
    rank0 = jnp.sum(jnp.where(hot0, cum_e, 0.0), axis=0, keepdims=True).astype(I32)
    rank1 = jnp.sum(jnp.where(hot1, cum_e, 0.0), axis=0, keepdims=True).astype(I32)
    at_rank = ones_where(lax.broadcasted_iota(I32, (ROW_CAP, tok), 0) == rank_b)
    high6 = jnp.where(in_block, (low // 64).astype(F32), 0.0).astype(BF)
    low6 = jnp.where(in_block, (low % 64).astype(F32), 0.0).astype(BF)
    nt = ((1,), (1,))
    asked = jnp.concatenate(
        [
            dot(high6, at_rank, nt),
            dot(low6, at_rank, nt),
            jnp.zeros((blocks, width - 2 * ROW_CAP), F32),
        ],
        axis=1,
    )
    first = lax.broadcasted_iota(I32, (8, width), 0) == 0
    for b in range(blocks):
        out_ref[b, routed:, :] = jnp.where(first, asked[b : b + 1, :], 0.0).astype(BF)
    slot_b = block * ROW_CAP + rank_b
    slot0 = e0 * CAP + rank0
    slot1 = e1 * CAP + rank1
    position = lax.broadcasted_iota(I32, (1, seq_len), 1)
    valid = jnp.concatenate(
        [jnp.where(position < len_ref[i], 1, 0) for i in range(seqs)], axis=1
    )
    zero = jnp.zeros((1, tok), F32)
    gw0 = gw_ref[0:1, :]
    gw1 = gw_ref[1:2, :]
    rows = jnp.concatenate(
        [
            slot_b.astype(F32),
            valid.astype(F32),
            slot0.astype(F32),
            slot1.astype(F32),
            gw0,
            gw1,
            zero,
            zero,
        ],
        axis=0,
    )
    rows_ref[...] = rows
    cols_ref[...] = rows.T
    d = d_ref[...]
    per = 4
    for b in range(0, blocks, per):
        at = lax.broadcasted_iota(I32, (per * routed, tok), 0) + b * routed
        m0 = at == slot0
        m1 = at == slot1
        moved = dot(ones_where(jnp.logical_or(m0, m1)), d)
        weight = jnp.sum(jnp.where(m0, gw0, jnp.where(m1, gw1, 0.0)), axis=1, keepdims=True)
        out_ref[b : b + per, :routed, :] = (weight * moved).astype(BF).reshape(per, routed, width)


def norm_body(rows_ref, cols_ref, gain_ref, got_ref, emb_ref, out_ref, emb_s, out_s, sems):
    tok, width = emb_s.shape
    blocks, cap, _ = got_ref.shape
    _, routed, _ = out_s.shape
    cols = cols_ref[...]
    rows = rows_ref[...]
    got = got_ref[...].reshape(blocks * cap, width)
    pick = ones_where(
        lax.broadcasted_iota(I32, (tok, blocks * cap), 1) == cols[:, 0:1].astype(I32)
    )
    embedded = jnp.where(cols[:, 1:2] > 0.0, dot(pick, got), 0.0)
    mean_square = jnp.mean(embedded * embedded, axis=1, keepdims=True)
    normed = (embedded * lax.rsqrt(mean_square + EPSILON) * gain_ref[...]).astype(BF)
    slot0 = rows[2:3, :].astype(I32)
    slot1 = rows[3:4, :].astype(I32)
    per = 4
    copies = []
    for n, i in enumerate(range(0, blocks, per)):
        at = lax.broadcasted_iota(I32, (per * routed, tok), 0) + i * routed
        sent = dot(ones_where(jnp.logical_or(at == slot0, at == slot1)), normed).astype(BF)
        out_s[i : i + per] = sent.reshape(per, routed, width)
        copies.append(pltpu.make_async_copy(out_s.at[pl.ds(i, per)], out_ref.at[pl.ds(i, per)], sems.at[n]))
        copies[-1].start()
    emb_s[...] = embedded.astype(BF)
    copies.append(pltpu.make_async_copy(emb_s, emb_ref, sems.at[blocks // per]))
    copies[-1].start()
    for c in copies:
        c.wait()


def expert_rows(ref, j):
    src, _, width = ref.shape
    return ref[:, j * CAP : (j + 1) * CAP, :].reshape(src * CAP, width)


def d_active_body(cot_ref, wd_ref, *outs):
    for j in range(wd_ref.shape[0]):
        cot = expert_rows(cot_ref, j)
        outs[j][...] = dot(cot, wd_ref[j]).astype(BF)
        outs[2 + j][...] = cot.T


def forward_body(j, *refs):
    x_ref, wg_ref, wu_ref, wd_ref, da_ref = refs[:5]
    out_ref, mid, xt, wg, wu, wd, das, outs, sin, sout = refs[-10:]
    _, _, width = outs.shape
    rows = das.shape[0]
    loads = [
        pltpu.make_async_copy(a, b, sin.at[n])
        for n, (a, b) in enumerate(
            ((wg_ref.at[j], wg), (wu_ref.at[j], wu), (wd_ref.at[j], wd), (da_ref, das))
        )
    ]
    for c in loads:
        c.start()
    step = 192
    per = step // CAP
    stores = []
    x = expert_rows(x_ref, j)
    xt[...] = x.T
    for i in range(rows // step):
        r = slice(i * step, (i + 1) * step)
        if i == 0:
            loads[0].wait()
        gate = dot(x[r], wg[...])
        if i == 0:
            loads[1].wait()
        up = dot(x[r], wu[...])
        sigmoid = jax.nn.sigmoid(gate)
        silu = gate * sigmoid
        active = (silu * up).astype(BF)
        if i == 0:
            loads[2].wait()
        out = dot(active, wd[...], ((1,), (1,))).astype(BF)
        outs[i * per : (i + 1) * per] = out.reshape(per, CAP, width)
        here = pl.ds(i * per, per)
        stores.append(
            pltpu.make_async_copy(outs.at[here], out_ref.at[here, pl.ds(j * CAP, CAP)], sout.at[i])
        )
        stores[-1].start()
        if i == 0:
            loads[3].wait()
        da = das[r].astype(F32)
        d_gate = (da * up * sigmoid * (1.0 + gate * (1.0 - sigmoid))).astype(BF)
        d_up = (da * silu).astype(BF)
        for g in range(8):
            c = slice(g * 128, (g + 1) * 128)
            mid[0, g, r, :] = active[:, c]
            mid[1, g, r, :] = d_gate[:, c]
            mid[2, g, r, :] = d_up[:, c]
    for c in stores:
        c.wait()


def products(pre_ref, first, ct_ref, xt_ref, mid_ref):
    for part in range(3):
        lt = (ct_ref if part == 0 else xt_ref)[...]
        for i in (0, 2):
            pair = jnp.concatenate(
                [mid_ref[part, pre_ref[first + i]], mid_ref[part, pre_ref[first + i + 1]]], axis=1
            )
            got = dot(lt, pair)
            yield part, i, got[:, :128]
            yield part, i + 1, got[:, 128:]


def send_body(pre_ref, ct_ref, xt_ref, mid_ref, out_ref):
    for part, i, block in products(pre_ref, 4, ct_ref, xt_ref, mid_ref):
        out_ref[part, i] = block.astype(BF)


def keep_body(
    pre_ref, ct_ref, xt_ref, mid_ref, got_ref, *refs
):
    asend, bsend = refs[2], refs[5]
    ao, an, bo, bn, sems = refs[6:]
    stores = [
        pltpu.make_async_copy(a, b, sems.at[n])
        for n, (a, b) in enumerate(zip((ao, an, bo, bn), (refs[0], refs[1], refs[3], refs[4])))
    ]
    for part, i, block in products(pre_ref, 0, ct_ref, xt_ref, mid_ref):
        total = (block + got_ref[part, i].astype(F32)).astype(BF)
        half = total.shape[0] // 2
        a, b = total[:half], total[half:]
        if i == 0:
            ao[part], bo[part] = a, b
        elif i == 1:
            asend[part, 0], bn[part] = a, b
        elif i == 2:
            asend[part, 1], bsend[part, 1] = a, b
        else:
            an[part], bsend[part, 0] = a, b
    for c in stores:
        c.start()
    for c in stores:
        c.wait()


def add_body(an, ar, bn, br, snd_a, snd_b):
    for keep, got, snd in ((an, ar, snd_a), (bn, br, snd_b)):
        snd[...] = (keep[...].astype(F32) + got[:, 1].astype(F32)).astype(BF)


def final_body(*refs):
    ins, outs = refs[:6], refs[-3:]
    for h in range(2):
        own, got, last = ins[3 * h : 3 * h + 3]
        for part, ref in enumerate(outs):
            half = ref.shape[1] // 2
            total = own[part].astype(F32) + got[part, 0].astype(F32) + last[part].astype(F32)
            ref[0, h * half : (h + 1) * half] = total


def combine_body(cols_ref, emb_ref, ret_ref, out_ref):
    tok = out_ref.shape[0]
    blocks, routed, width = ret_ref.shape
    cols = cols_ref[...]
    ret = ret_ref[...].reshape(blocks * routed, width)
    at = lax.broadcasted_iota(I32, (tok, blocks * routed), 1)
    first = dot(ones_where(at == cols[:, 2:3].astype(I32)), ret)
    second = dot(ones_where(at == cols[:, 3:4].astype(I32)), ret)
    mixed = emb_ref[...].astype(F32) + (cols[:, 4:5] * first + cols[:, 5:6] * second)
    out_ref[...] = mixed.astype(BF)


def exchange(x):
    return lax.all_to_all(x, "ex", split_axis=0, concat_axis=0, tiled=True)


def layer(
    item_ids, lengths, expert_ids, gate_weights, table, norm_gain, w_gate, w_up, w_down, d_out
):
    ex_count = lax.axis_size("ex")
    seqs_here, seq_len = item_ids.shape
    tok = seqs_here * seq_len
    width = table.shape[1]
    exp_here, _, ff = w_gate.shape
    routed = exp_here * CAP
    rows_e = ex_count * CAP
    vmem = pl.BlockSpec(memory_space=pltpu.VMEM)
    smem = pl.BlockSpec(memory_space=pltpu.SMEM)
    hbm = pl.BlockSpec(memory_space=pltpu.HBM)
    dma = pltpu.SemaphoreType.DMA

    outbound, rows, cols = call(
        index_body,
        (
            shape((ex_count, routed + 8, width), BF),
            shape((8, tok), F32),
            shape((tok, 8), F32),
        ),
        56,
        in_specs=[smem] + [vmem] * 4,
        out_specs=(vmem,) * 3,
    )(lengths, item_ids, expert_ids.T, gate_weights.T, d_out)
    inbound = exchange(outbound)
    asked = inbound[:, routed, : 2 * ROW_CAP].astype(F32)
    asked = (asked[:, :ROW_CAP] * 64.0 + asked[:, ROW_CAP:]).astype(I32)
    picked = jnp.take(table, asked.reshape(-1), axis=0, mode="clip")
    got = exchange(picked.reshape(ex_count, ROW_CAP, width))
    embedded, send_rows = call(
        norm_body,
        (pltpu.HBM((tok, width), BF), pltpu.HBM((ex_count, routed, width), BF)),
        14,
        in_specs=[vmem] * 4,
        out_specs=(hbm,) * 2,
        scratch_shapes=[
            pltpu.VMEM((tok, width), BF),
            pltpu.VMEM((ex_count, routed, width), BF),
            dma((5,)),
        ],
    )(rows, cols, norm_gain[None, :], got)
    in_rows = exchange(send_rows)
    turned = shape((width, rows_e), BF)
    *d_active, ct0, ct1 = call(
        d_active_body,
        (shape((rows_e, ff), BF),) * exp_here + (turned,) * exp_here,
        56,
        in_specs=[vmem] * 2,
        out_specs=(vmem,) * (2 * exp_here),
    )(*stay(inbound, w_down))

    me = lax.axis_index("grp")
    place = jnp.arange(8, dtype=I32)
    pre = jnp.bitwise_xor(me // 2, place % 4) * 2 + jnp.bitwise_xor(me % 2, place // 4)
    core = [(g, g ^ 1) for g in range(8)]
    near1 = [(g, g ^ 2) for g in range(8)]
    near3 = [(g, g ^ 6) for g in range(8)]

    def forward(j, back):
        return call(
            lambda *refs: forward_body(j, *refs),
            (
                pltpu.HBM((ex_count, routed, width), BF),
                shape((3, 8, rows_e, 128), BF),
                turned,
            ),
            14,
            in_specs=[vmem] + [hbm] * (4 + len(back)),
            out_specs=(hbm, vmem, vmem),
            input_output_aliases={5: 0} if back else {},
            scratch_shapes=[
                pltpu.VMEM((width, ff), BF),
                pltpu.VMEM((width, ff), BF),
                pltpu.VMEM((width, ff), BF),
                pltpu.VMEM((rows_e, ff), BF),
                pltpu.VMEM((ex_count, CAP, width), BF),
                dma((4,)),
                dma((4,)),
            ],
        )(in_rows, *stay(w_gate, w_up, w_down, d_active[j], *back))

    def send(j, pre, mid, xt):
        sent = call(
            send_body,
            shape((3, 4, width, 128), BF),
            6,
            in_specs=[smem] + [vmem] * 3,
            out_specs=vmem,
        )(pre, (ct0, ct1)[j], xt, mid)
        return sent, lax.ppermute(sent, "grp", core)

    piece = shape((3, width // 2, 128), BF)
    own = pltpu.HBM((3, width // 2, 128), BF)
    pair = shape((3, 2, width // 2, 128), BF)

    def keep(j, pre, mid, xt, crossed):
        ao, an, asend, bo, bn, bsend = call(
            keep_body,
            (own, own, pair) * 2,
            6,
            in_specs=[smem] + [vmem] * 4,
            out_specs=(hbm, hbm, vmem) * 2,
            scratch_shapes=[pltpu.VMEM((3, width // 2, 128), BF)] * 4 + [dma((4,))],
        )(pre, (ct0, ct1)[j], xt, mid, crossed)
        ar = lax.ppermute(asend, "grp", near1)
        br = lax.ppermute(bsend, "grp", near3)
        return ao, an, ar, bo, bn, br

    def add(ao, an, ar, bo, bn, br):
        snd_a, snd_b = call(
            add_body, (piece,) * 2, 6, in_specs=[vmem] * 4, out_specs=(vmem,) * 2
        )(an, ar, bn, br)
        a_last = lax.ppermute(snd_a, "grp", near3)
        b_last = lax.ppermute(snd_b, "grp", near1)
        return ao, ar, a_last, bo, br, b_last

    def final(j, pieces, grads):
        return call(
            final_body,
            (shape((exp_here, width, 128), F32),) * 3,
            8,
            grid=(1,),
            in_specs=[vmem] * 6 + [hbm] * len(grads),
            out_specs=(pl.BlockSpec((1, width, 128), lambda _, j=j: (j, 0, 0)),) * 3,
            input_output_aliases={6 + i: i for i in range(3)} if grads else {},
        )(*pieces, *grads)

    bar = lax.optimization_barrier
    back, mid0, xt0 = forward(0, ())
    sent0, crossed0 = send(0, pre, mid0, xt0)
    back, _ = bar((back, sent0))
    back, mid1, xt1 = forward(1, (back,))
    sent1, crossed1 = send(1, pre, mid1, xt1)
    pre0, _ = bar((pre, sent1))
    kept0 = keep(0, pre0, mid0, xt0, crossed0)
    pre1, _ = bar((pre, kept0[0]))
    kept1 = keep(1, pre1, mid1, xt1, crossed1)
    back, _ = bar((back, kept1[0]))
    returned = exchange(back)
    grads = final(0, add(*kept0), ())
    grad_down, grad_gate, grad_up = final(1, add(*kept1), grads)
    output = call(
        combine_body, shape((tok, width), BF), 12, in_specs=[vmem] * 3, out_specs=vmem
    )(cols, embedded, returned)
    return (output, grad_gate, grad_up, grad_down)


def solution(mesh):
    placed = (
        P(("grp", "ex"), None),
        P(("grp", "ex")),
        P(("grp", "ex"), None),
        P(("grp", "ex"), None),
        P("ex", None),
        P(),
        P("ex", None, None),
        P("ex", None, None),
        P("ex", None, None),
        P(("grp", "ex"), None),
    )
    return jax.shard_map(
        layer,
        mesh=mesh,
        in_specs=placed,
        out_specs=(
            P(("grp", "ex"), None),
            P("ex", None, "grp"),
            P("ex", None, "grp"),
            P("ex", None, "grp"),
        ),
        check_vma=False,
    )
```

profile of v0, /device:TPU:0, one launch (start us, length us, event | category | flops | bytes accessed | tf_op | source)
XLA Modules:
  0.0 171.6 jit_solution(5369572870567324545)
XLA Ops:
  0.6 4.2 %shard_map.129 = (bf16[16,104,512]{2,1,0:T(8,128)(2,1)}, f32[8,512]{1,0:T(8,128)}, f32[512,8]{1,0:T(8,128)}) custom-call(s32[2]{0:T(128)} %len_ref.1, s32[2,256]{1,0:T(2,128)} %ids_ref.1, s32[2,512]{1,0:T(2,128)} %bitcast.14, f32[2,512]{1,0:T(2,128)} %bitcast.15, bf16[512,512]{1,0:T(8,128)(2,1)} %d_ref.1), custom_call_target="tpu_custom_call" | custom-call | tf_op jit(solution)/shard_map/pallas_call | solution.py:301
  4.8 32.3 %all_to_all.20.cot_ref = bf16[16,104,512]{2,1,0:T(8,128)(2,1)S(1)} all-to-all(bf16[16,104,512]{2,1,0:T(8,128)(2,1)} %get-tuple-element.47), channel_id=1, replica_groups=mesh['grp'=8,'ex'=16] {'ex'}, dimensions={0} | all-to-all | bytes 3407872 | tf_op jit(solution)/shard_map/all_to_all | solution.py:283
  37.2 1.2 copy-done.16
  38.4 10.3 %gather_fusion = bf16[2048,512]{1,0:T(8,128)(2,1)S(1)} fusion(bf16[4096,512]{1,0:T(8,128)(2,1)} %param.14, s32[2048]{0:T(1024)S(1)} %fusion.2), kind=kCustom, calls=%fused_computation | custom fusion | bytes 4202496 | tf_op jit(solution)/shard_map/jit(_take)/gather | solution.py:315
  48.7 30.8 %all_to_all.21.got_ref = bf16[16,128,512]{2,1,0:T(8,128)(2,1)S(1)} all-to-all(bf16[16,128,512]{2,1,0:T(8,128)(2,1)S(1)} %bitcast.12), channel_id=1, replica_groups=mesh['grp'=8,'ex'=16] {'ex'}, dimensions={0} | all-to-all | bytes 4194304 | tf_op jit(solution)/shard_map/all_to_all | solution.py:283
  79.5 3.3 %shard_map.130 = (bf16[512,512]{1,0:T(8,128)(2,1)}, bf16[16,96,512]{2,1,0:T(8,128)(2,1)}) custom-call(f32[8,512]{1,0:T(8,128)S(1)} %copy-done.12, f32[512,8]{1,0:T(8,128)S(1)} %copy-done.2, f32[1,512]{1,0:T(1,128)S(1)} %bitcast.11, bf16[16,128,512]{2,1,0:T(8,128)(2,1)S(1)} %all_to_all.21.got_ref), custom_call_target="tpu_custom_call" | custom-call | tf_op jit(solution)/shard_map/pallas_call | solution.py:317
  82.9 3.9 %all-to-all-start.2 = ((bf16[16,96,512]{2,1,0:T(8,128)(2,1)}), bf16[16,96,512]{2,1,0:T(8,128)(2,1)S(1)}, u32[]{:S(2)}, u32[]{:S(2)}) async-start(bf16[16,96,512]{2,1,0:T(8,128)(2,1)} %get-tuple-element.49), calls=%async_computation.2 | async-start | bytes 3145728 | tf_op jit(solution)/shard_map/all_to_all | solution.py:283
  86.8 5.6 %shard_map.131 = (bf16[768,1024]{1,0:T(8,128)(2,1)}, bf16[768,1024]{1,0:T(8,128)(2,1)}, bf16[512,768]{1,0:T(8,128)(2,1)}, bf16[512,768]{1,0:T(8,128)(2,1)}) custom-call(bf16[16,104,512]{2,1,0:T(8,128)(2,1)} %copy-done.16, bf16[2,512,1024]{2,1,0:T(8,128)(2,1)} %refs_3_.3), custom_call_target="tpu_custom_call" | custom-call | tf_op jit(solution)/shard_map/pallas_call | solution.py:331
  92.4 15.9 %all-to-all-done.2.refs_0_ = bf16[16,96,512]{2,1,0:T(8,128)(2,1)S(1)} async-done(((bf16[16,96,512]{2,1,0:T(8,128)(2,1)}), bf16[16,96,512]{2,1,0:T(8,128)(2,1)S(1)}, u32[]{:S(2)}, u32[]{:S(2)}) %all-to-all-start.2) | async-done | bytes 1572896 | tf_op jit(solution)/shard_map/all_to_all | solution.py:283
  108.3 6.9 %shard_map.132 = (bf16[16,96,512]{2,1,0:T(8,128)(2,1)}, bf16[3,8,768,128]{3,2,1,0:T(8,128)(2,1)S(1)}, bf16[512,768]{1,0:T(8,128)(2,1)S(1)}) custom-call(bf16[16,96,512]{2,1,0:T(8,128)(2,1)S(1)} %all-to-all-done.2.refs_0_, bf16[2,512,1024]{2,1,0:T(8,128)(2,1)} %refs_1_.3, bf16[2,512,1024]{2,1,0:T(8,128)(2,1)} %refs_2_.3, bf16[2,512,1024]{2,1,0:T(8,128)(2,1)} %refs_3_.3, ...), custom_call_target="tpu_custom_call" | custom-call | tf_op jit(solution)/shard_map/pallas_call | solution.py:347
  115.2 1.9 %shard_map.133 = bf16[3,4,512,128]{3,2,1,0:T(8,128)(2,1)S(1)} custom-call(s32[8]{0:T(128)S(1)} %fusion.5.pre_ref, bf16[512,768]{1,0:T(8,128)(2,1)S(1)} %copy-done.1, bf16[512,768]{1,0:T(8,128)(2,1)S(1)} %get-tuple-element.54.xt_ref, bf16[3,8,768,128]{3,2,1,0:T(8,128)(2,1)S(1)} %get-tuple-element.55.mid_ref), custom_call_target="tpu_custom_call" | custom-call | tf_op jit(solution)/shard_map/pallas_call | solution.py:370
  117.5 6.9 %shard_map.134 = (bf16[16,96,512]{2,1,0:T(8,128)(2,1)}, bf16[3,8,768,128]{3,2,1,0:T(8,128)(2,1)S(1)}, bf16[512,768]{1,0:T(8,128)(2,1)S(1)}) custom-call(bf16[16,96,512]{2,1,0:T(8,128)(2,1)S(1)} %all-to-all-done.2.refs_0_, bf16[2,512,1024]{2,1,0:T(8,128)(2,1)} %refs_1_.3, bf16[2,512,1024]{2,1,0:T(8,128)(2,1)} %refs_2_.3, ...), custom_call_target="tpu_custom_call", output_to_operand_aliasing={{0}: (5, {})} | custom-call | tf_op jit(solution)/shard_map/pallas_call | solution.py:347
  124.4 1.9 %shard_map.135 = bf16[3,4,512,128]{3,2,1,0:T(8,128)(2,1)S(1)} custom-call(s32[8]{0:T(128)S(1)} %fusion.5.pre_ref, bf16[512,768]{1,0:T(8,128)(2,1)S(1)} %copy-done, bf16[512,768]{1,0:T(8,128)(2,1)S(1)} %get-tuple-element.59.xt_ref, bf16[3,8,768,128]{3,2,1,0:T(8,128)(2,1)S(1)} %get-tuple-element.60.mid_ref), custom_call_target="tpu_custom_call" | custom-call | tf_op jit(solution)/shard_map/pallas_call | solution.py:370
  126.3 0.6 collective-permute-start.1
  126.9 2.8 %shard_map.136 = (bf16[3,256,128]{2,1,0:T(8,128)(2,1)}, bf16[3,256,128]{2,1,0:T(8,128)(2,1)}, bf16[3,2,256,128]{3,2,1,0:T(8,128)(2,1)S(1)}, bf16[3,256,128]{2,1,...) custom-call(s32[8]{0:T(128)S(1)} %fusion.5.pre_ref, bf16[512,768]{1,0:T(8,128)(2,1)S(1)} %copy-done.1, ...), custom_call_target="tpu_custom_call" | custom-call | tf_op jit(solution)/shard_map/pallas_call | solution.py:384
  129.9 2.8 %shard_map.137 = (bf16[3,256,128]{2,1,0:T(8,128)(2,1)}, bf16[3,256,128]{2,1,0:T(8,128)(2,1)}, bf16[3,2,256,128]{3,2,1,0:T(8,128)(2,1)S(1)}, bf16[3,256,128]{2,1,...) custom-call(s32[8]{0:T(128)S(1)} %fusion.5.pre_ref, bf16[512,768]{1,0:T(8,128)(2,1)S(1)} %copy-done, ...), custom_call_target="tpu_custom_call" | custom-call | tf_op jit(solution)/shard_map/pallas_call | solution.py:384
  132.8 3.9 %all-to-all-start.3 = ((bf16[16,96,512]{2,1,0:T(8,128)(2,1)}), bf16[16,96,512]{2,1,0:T(8,128)(2,1)S(1)}, u32[]{:S(2)}, u32[]{:S(2)}) async-start(bf16[16,96,512]{2,1,0:T(8,128)(2,1)} %get-tuple-element.65), calls=%async_computation.3 | async-start | bytes 3145728 | tf_op jit(solution)/shard_map/all_to_all | solution.py:283
  136.6 1.6 collective-permute-start.6
  138.2 2.1 %collective-permute-start.7 = (bf16[3,2,256,128]{3,2,1,0:T(8,128)(2,1)}, bf16[3,2,256,128]{3,2,1,0:T(8,128)(2,1)S(1)}, u32[]{:S(2)}, u32[]{:S(2)}) collective-permute-start(bf16[3,2,256,128]{3,2,1,0:T(8,128)(2,1)} %copy-done.14), channel_id=1, source_target_pairs={{0,96},{16,112},{32,64},{48,80},{64,32},{80,48},{96,0},{112,16},{1... | collective-permute-start | bytes 1179656 | tf_op jit(solution)/shard_map/ppermute | solution.py:393
  140.3 0.6 collective-permute-start.2
  140.9 0.6 collective-permute-start.3
  141.5 7.4 %collective-permute-done.6.ar.refs_1_ = bf16[3,2,256,128]{3,2,1,0:T(8,128)(2,1)S(1)} collective-permute-done((bf16[3,2,256,128]{3,2,1,0:T(8,128)(2,1)}, bf16[3,2,256,128]{3,2,1,0:T(8,128)(2,1)S(1)}, u32[]{:S(2)}, u32[]{:S(2)}) %collective-permute-start.6) | collective-permute-done | bytes 393248 | tf_op jit(solution)/shard_map/ppermute | solution.py:392
  148.9 2.7 %collective-permute-done.7.br.refs_4_ = bf16[3,2,256,128]{3,2,1,0:T(8,128)(2,1)S(1)} collective-permute-done((bf16[3,2,256,128]{3,2,1,0:T(8,128)(2,1)}, bf16[3,2,256,128]{3,2,1,0:T(8,128)(2,1)S(1)}, u32[]{:S(2)}, u32[]{:S(2)}) %collective-permute-start.7) | collective-permute-done | bytes 393248 | tf_op jit(solution)/shard_map/ppermute | solution.py:393
  151.7 2.2 %collective-permute-start.8 = (bf16[3,256,128]{2,1,0:T(8,128)(2,1)S(1)}, bf16[3,256,128]{2,1,0:T(8,128)(2,1)S(1)}, u32[]{:S(2)}, u32[]{:S(2)}) collective-permute-start(bf16[3,256,128]{2,1,0:T(8,128)(2,1)S(1)} %get-tuple-element.77), channel_id=1, source_target_pairs={{0,96},{16,112},{32,64},{48,80},{64,32},{80,48},{96,0},{112,16},{1... | collective-permute-start | bytes 589832 | tf_op jit(solution)/shard_map/ppermute | solution.py:400
  153.9 3.4 %collective-permute-done.2.ar.refs_1_ = bf16[3,2,256,128]{3,2,1,0:T(8,128)(2,1)S(1)} collective-permute-done((bf16[3,2,256,128]{3,2,1,0:T(8,128)(2,1)S(1)}, bf16[3,2,256,128]{3,2,1,0:T(8,128)(2,1)S(1)}, u32[]{:S(2)}, u32[]{:S(2)}) %collective-permute-start.2) | collective-permute-done | bytes 393248 | tf_op jit(solution)/shard_map/ppermute | solution.py:392
  157.3 2.7 %collective-permute-done.3.br.refs_4_ = bf16[3,2,256,128]{3,2,1,0:T(8,128)(2,1)S(1)} collective-permute-done((bf16[3,2,256,128]{3,2,1,0:T(8,128)(2,1)S(1)}, bf16[3,2,256,128]{3,2,1,0:T(8,128)(2,1)S(1)}, u32[]{:S(2)}, u32[]{:S(2)}) %collective-permute-start.3) | collective-permute-done | bytes 393248 | tf_op jit(solution)/shard_map/ppermute | solution.py:393
  160.1 2.2 %collective-permute-start.4 = (bf16[3,256,128]{2,1,0:T(8,128)(2,1)S(1)}, bf16[3,256,128]{2,1,0:T(8,128)(2,1)S(1)}, u32[]{:S(2)}, u32[]{:S(2)}) collective-permute-start(bf16[3,256,128]{2,1,0:T(8,128)(2,1)S(1)} %get-tuple-element.70), channel_id=1, source_target_pairs={{0,96},{16,112},{32,64},{48,80},{64,32},{80,48},{96,0},{112,16},{1... | collective-permute-start | bytes 589832 | tf_op jit(solution)/shard_map/ppermute | solution.py:400
  162.4 1.9 %collective-permute-done.8.refs_2_ = bf16[3,256,128]{2,1,0:T(8,128)(2,1)S(1)} collective-permute-done((bf16[3,256,128]{2,1,0:T(8,128)(2,1)S(1)}, bf16[3,256,128]{2,1,0:T(8,128)(2,1)S(1)}, u32[]{:S(2)}, u32[]{:S(2)}) %collective-permute-start.8) | collective-permute-done | bytes 196640 | tf_op jit(solution)/shard_map/ppermute | solution.py:400
  164.3 0.9 shard_map.141
  165.2 2.4 %collective-permute-done.4.refs_2_ = bf16[3,256,128]{2,1,0:T(8,128)(2,1)S(1)} collective-permute-done((bf16[3,256,128]{2,1,0:T(8,128)(2,1)S(1)}, bf16[3,256,128]{2,1,0:T(8,128)(2,1)S(1)}, u32[]{:S(2)}, u32[]{:S(2)}) %collective-permute-start.4) | collective-permute-done | bytes 196640 | tf_op jit(solution)/shard_map/ppermute | solution.py:400
  168.0 0.9 shard_map.142
  169.0 2.7 %shard_map.138 = bf16[512,512]{1,0:T(8,128)(2,1)} custom-call(f32[512,8]{1,0:T(8,128)S(1)} %copy-done.2, bf16[512,512]{1,0:T(8,128)(2,1)S(1)} %copy-done.3, bf16[16,96,512]{2,1,0:T(8,128)(2,1)S(1)} %all-to-all-done.3.ret_ref), custom_call_target="tpu_custom_call" | custom-call | tf_op jit(solution)/shard_map/pallas_call | solution.py:429
  (47 shorter events, 1.2 us)
Async XLA Ops:
  37.1 1.2 copy-start.16
  48.7 30.8 %copy-start.2 = (f32[512,8]{1,0:T(8,128)S(1)}, f32[512,8]{1,0:T(8,128)}, u32[]{:S(2)}) copy-start(f32[512,8]{1,0:T(8,128)} %get-tuple-element.45.cols_ref) | copy-start | bytes 49156
  48.7 30.8 %copy-start.12 = (f32[8,512]{1,0:T(8,128)S(1)}, f32[8,512]{1,0:T(8,128)}, u32[]{:S(2)}) copy-start(f32[8,512]{1,0:T(8,128)} %get-tuple-element.46.rows_ref) | copy-start | bytes 49156
  48.7 30.8 %copy-start.13 = (f32[512]{0:T(512)S(1)}, f32[512]{0:T(512)}, u32[]{:S(2)}) copy-start(f32[512]{0:T(512)} %param.15) | copy-start | bytes 6148
  82.9 25.4 %all-to-all-start.2 = ((bf16[16,96,512]{2,1,0:T(8,128)(2,1)}), bf16[16,96,512]{2,1,0:T(8,128)(2,1)S(1)}, u32[]{:S(2)}, u32[]{:S(2)}) async-start(bf16[16,96,512]{2,1,0:T(8,128)(2,1)} %get-tuple-element.49), calls=%async_computation.2 | async-start | bytes 3145728 | tf_op jit(solution)/shard_map/all_to_all | solution.py:283
  108.3 6.9 %copy-start.1 = (bf16[512,768]{1,0:T(8,128)(2,1)S(1)}, bf16[512,768]{1,0:T(8,128)(2,1)}, u32[]{:S(2)}) copy-start(bf16[512,768]{1,0:T(8,128)(2,1)} %get-tuple-element.53.ct_ref) | copy-start | bytes 2359300
  117.1 9.7 %collective-permute-start = (bf16[3,4,512,128]{3,2,1,0:T(8,128)(2,1)S(1)}, bf16[3,4,512,128]{3,2,1,0:T(8,128)(2,1)S(1)}, u32[]{:S(2)}, u32[]{:S(2)}) collective-permute-start(bf16[3,4,512,128]{3,2,1,0:T(8,128)(2,1)S(1)} %shard_map.133), channel_id=1, source_target_pairs={{0,16},{16,0},{32,48},{48,32},{64,80},{80,64},{96,112},{112,96},{1... | collective-permute-start | bytes 4718600 | tf_op jit(solution)/shard_map/ppermute | solution.py:377
  117.5 6.9 %copy-start = (bf16[512,768]{1,0:T(8,128)(2,1)S(1)}, bf16[512,768]{1,0:T(8,128)(2,1)}, u32[]{:S(2)}) copy-start(bf16[512,768]{1,0:T(8,128)(2,1)} %get-tuple-element.58.ct_ref) | copy-start | bytes 2359300
  126.3 3.6 %collective-permute-start.1 = (bf16[3,4,512,128]{3,2,1,0:T(8,128)(2,1)S(1)}, bf16[3,4,512,128]{3,2,1,0:T(8,128)(2,1)S(1)}, u32[]{:S(2)}, u32[]{:S(2)}) collective-permute-start(bf16[3,4,512,128]{3,2,1,0:T(8,128)(2,1)S(1)} %shard_map.135), channel_id=1, source_target_pairs={{0,16},{16,0},{32,48},{48,32},{64,80},{80,64},{96,112},{112,96},{1... | collective-permute-start | bytes 4718600 | tf_op jit(solution)/shard_map/ppermute | solution.py:377
  129.7 3.0 %copy-start.14 = (bf16[3,2,256,128]{3,2,1,0:T(8,128)(2,1)}, bf16[3,2,256,128]{3,2,1,0:T(8,128)(2,1)S(1)}, u32[]{:S(2)}) copy-start(bf16[3,2,256,128]{3,2,1,0:T(8,128)(2,1)S(1)} %get-tuple-element.76) | copy-start | bytes 1179652
  129.7 3.0 %copy-start.15 = (bf16[3,2,256,128]{3,2,1,0:T(8,128)(2,1)}, bf16[3,2,256,128]{3,2,1,0:T(8,128)(2,1)S(1)}, u32[]{:S(2)}) copy-start(bf16[3,2,256,128]{3,2,1,0:T(8,128)(2,1)S(1)} %get-tuple-element.73) | copy-start | bytes 1179652
  132.7 18.9 %copy-start.10 = (bf16[3,256,128]{2,1,0:T(8,128)(2,1)S(1)}, bf16[3,256,128]{2,1,0:T(8,128)(2,1)}, u32[]{:S(2)}) copy-start(bf16[3,256,128]{2,1,0:T(8,128)(2,1)} %get-tuple-element.74.an) | copy-start | bytes 589828
  132.7 18.9 %copy-start.11 = (bf16[3,256,128]{2,1,0:T(8,128)(2,1)S(1)}, bf16[3,256,128]{2,1,0:T(8,128)(2,1)}, u32[]{:S(2)}) copy-start(bf16[3,256,128]{2,1,0:T(8,128)(2,1)} %get-tuple-element.75.bn) | copy-start | bytes 589828
  132.7 27.3 %copy-start.8 = (bf16[3,256,128]{2,1,0:T(8,128)(2,1)S(1)}, bf16[3,256,128]{2,1,0:T(8,128)(2,1)}, u32[]{:S(2)}) copy-start(bf16[3,256,128]{2,1,0:T(8,128)(2,1)} %get-tuple-element.67.an) | copy-start | bytes 589828
  132.7 27.3 %copy-start.9 = (bf16[3,256,128]{2,1,0:T(8,128)(2,1)S(1)}, bf16[3,256,128]{2,1,0:T(8,128)(2,1)}, u32[]{:S(2)}) copy-start(bf16[3,256,128]{2,1,0:T(8,128)(2,1)} %get-tuple-element.68.bn) | copy-start | bytes 589828
  132.8 36.2 %all-to-all-start.3 = ((bf16[16,96,512]{2,1,0:T(8,128)(2,1)}), bf16[16,96,512]{2,1,0:T(8,128)(2,1)S(1)}, u32[]{:S(2)}, u32[]{:S(2)}) async-start(bf16[16,96,512]{2,1,0:T(8,128)(2,1)} %get-tuple-element.65), calls=%async_computation.3 | async-start | bytes 3145728 | tf_op jit(solution)/shard_map/all_to_all | solution.py:283
  136.6 27.6 %copy-start.6 = (bf16[3,256,128]{2,1,0:T(8,128)(2,1)S(1)}, bf16[3,256,128]{2,1,0:T(8,128)(2,1)}, u32[]{:S(2)}) copy-start(bf16[3,256,128]{2,1,0:T(8,128)(2,1)} %get-tuple-element.62.refs_0_) | copy-start | bytes 589828
  136.6 27.6 %copy-start.7 = (bf16[3,256,128]{2,1,0:T(8,128)(2,1)S(1)}, bf16[3,256,128]{2,1,0:T(8,128)(2,1)}, u32[]{:S(2)}) copy-start(bf16[3,256,128]{2,1,0:T(8,128)(2,1)} %get-tuple-element.78.refs_3_) | copy-start | bytes 589828
  136.6 12.3 %collective-permute-start.6 = (bf16[3,2,256,128]{3,2,1,0:T(8,128)(2,1)}, bf16[3,2,256,128]{3,2,1,0:T(8,128)(2,1)S(1)}, u32[]{:S(2)}, u32[]{:S(2)}) collective-permute-start(bf16[3,2,256,128]{3,2,1,0:T(8,128)(2,1)} %copy-done.15), channel_id=1, source_target_pairs={{0,32},{16,48},{32,0},{48,16},{64,96},{80,112},{96,64},{112,80},{1... | collective-permute-start | bytes 1179656 | tf_op jit(solution)/shard_map/ppermute | solution.py:392
  138.2 13.4 %collective-permute-start.7 = (bf16[3,2,256,128]{3,2,1,0:T(8,128)(2,1)}, bf16[3,2,256,128]{3,2,1,0:T(8,128)(2,1)S(1)}, u32[]{:S(2)}, u32[]{:S(2)}) collective-permute-start(bf16[3,2,256,128]{3,2,1,0:T(8,128)(2,1)} %copy-done.14), channel_id=1, source_target_pairs={{0,96},{16,112},{32,64},{48,80},{64,32},{80,48},{96,0},{112,16},{1... | collective-permute-start | bytes 1179656 | tf_op jit(solution)/shard_map/ppermute | solution.py:393
  140.3 17.0 %collective-permute-start.2 = (bf16[3,2,256,128]{3,2,1,0:T(8,128)(2,1)S(1)}, bf16[3,2,256,128]{3,2,1,0:T(8,128)(2,1)S(1)}, u32[]{:S(2)}, u32[]{:S(2)}) collective-permute-start(bf16[3,2,256,128]{3,2,1,0:T(8,128)(2,1)S(1)} %get-tuple-element.66), channel_id=1, source_target_pairs={{0,32},{16,48},{32,0},{48,16},{64,96},{80,112},{96,64},{112,80},{1... | collective-permute-start | bytes 1179656 | tf_op jit(solution)/shard_map/ppermute | solution.py:392
  140.9 19.1 %collective-permute-start.3 = (bf16[3,2,256,128]{3,2,1,0:T(8,128)(2,1)S(1)}, bf16[3,2,256,128]{3,2,1,0:T(8,128)(2,1)S(1)}, u32[]{:S(2)}, u32[]{:S(2)}) collective-permute-start(bf16[3,2,256,128]{3,2,1,0:T(8,128)(2,1)S(1)} %get-tuple-element.69), channel_id=1, source_target_pairs={{0,96},{16,112},{32,64},{48,80},{64,32},{80,48},{96,0},{112,16},{1... | collective-permute-start | bytes 1179656 | tf_op jit(solution)/shard_map/ppermute | solution.py:393
  151.6 16.4 %copy-start.4 = (bf16[3,256,128]{2,1,0:T(8,128)(2,1)S(1)}, bf16[3,256,128]{2,1,0:T(8,128)(2,1)}, u32[]{:S(2)}) copy-start(bf16[3,256,128]{2,1,0:T(8,128)(2,1)} %get-tuple-element.64.refs_0_) | copy-start | bytes 589828
  151.6 16.4 %copy-start.5 = (bf16[3,256,128]{2,1,0:T(8,128)(2,1)S(1)}, bf16[3,256,128]{2,1,0:T(8,128)(2,1)}, u32[]{:S(2)}) copy-start(bf16[3,256,128]{2,1,0:T(8,128)(2,1)} %get-tuple-element.71.refs_3_) | copy-start | bytes 589828
  151.7 12.5 %collective-permute-start.8 = (bf16[3,256,128]{2,1,0:T(8,128)(2,1)S(1)}, bf16[3,256,128]{2,1,0:T(8,128)(2,1)S(1)}, u32[]{:S(2)}, u32[]{:S(2)}) collective-permute-start(bf16[3,256,128]{2,1,0:T(8,128)(2,1)S(1)} %get-tuple-element.77), channel_id=1, source_target_pairs={{0,96},{16,112},{32,64},{48,80},{64,32},{80,48},{96,0},{112,16},{1... | collective-permute-start | bytes 589832 | tf_op jit(solution)/shard_map/ppermute | solution.py:400
  153.9 10.3 %collective-permute-start.9 = (bf16[3,256,128]{2,1,0:T(8,128)(2,1)S(1)}, bf16[3,256,128]{2,1,0:T(8,128)(2,1)S(1)}, u32[]{:S(2)}, u32[]{:S(2)}) collective-permute-start(bf16[3,256,128]{2,1,0:T(8,128)(2,1)S(1)} %get-tuple-element.79), channel_id=1, source_target_pairs={{0,32},{16,48},{32,0},{48,16},{64,96},{80,112},{96,64},{112,80},{1... | collective-permute-start | bytes 589832 | tf_op jit(solution)/shard_map/ppermute | solution.py:401
  160.1 7.5 %collective-permute-start.4 = (bf16[3,256,128]{2,1,0:T(8,128)(2,1)S(1)}, bf16[3,256,128]{2,1,0:T(8,128)(2,1)S(1)}, u32[]{:S(2)}, u32[]{:S(2)}) collective-permute-start(bf16[3,256,128]{2,1,0:T(8,128)(2,1)S(1)} %get-tuple-element.70), channel_id=1, source_target_pairs={{0,96},{16,112},{32,64},{48,80},{64,32},{80,48},{96,0},{112,16},{1... | collective-permute-start | bytes 589832 | tf_op jit(solution)/shard_map/ppermute | solution.py:400
  162.3 5.7 %collective-permute-start.5 = (bf16[3,256,128]{2,1,0:T(8,128)(2,1)S(1)}, bf16[3,256,128]{2,1,0:T(8,128)(2,1)S(1)}, u32[]{:S(2)}, u32[]{:S(2)}) collective-permute-start(bf16[3,256,128]{2,1,0:T(8,128)(2,1)S(1)} %get-tuple-element.72), channel_id=1, source_target_pairs={{0,32},{16,48},{32,0},{48,16},{64,96},{80,112},{96,64},{112,80},{1... | collective-permute-start | bytes 589832 | tf_op jit(solution)/shard_map/ppermute | solution.py:401
  165.2 3.8 %copy-start.3 = (bf16[512,512]{1,0:T(8,128)(2,1)S(1)}, bf16[512,512]{1,0:T(8,128)(2,1)}, u32[]{:S(2)}) copy-start(bf16[512,512]{1,0:T(8,128)(2,1)} %get-tuple-element.48.emb_ref) | copy-start | bytes 1572868
where the time goes:
time: 172 us
  blocking collectives  63.1 us (37%)
  Pallas kernels  41 us (24%)
  waiting for transfers between devices  37 us (22%)
  starting transfers between devices  17.9 us (10%)
  local copies, waits for them, and re-layouts  11.6 us (7%)
    all_to_all x2, blocking collectives, exchange(): return lax.all_to_all(x, 'ex', split_axis=0, concat_axis=0, tiled=True)  63.1 us
    all_to_all x2, waiting for transfers between devices, exchange(): return lax.all_to_all(x, 'ex', split_axis=0, concat_axis=0, tiled=True)  15.9 us
    pallas_call x2, Pallas kernels, forward(): call(lambda *refs: forward_body(j, *refs), (pltpu.HBM((ex_count, routed,...  13.7 us
    ppermute x2, waiting for transfers between devices, keep(): ar = lax.ppermute(asend, 'grp', near1)  10.8 us
    gather x1, local copies, waits for them, and re-layouts, layer(): picked = jnp.take(table, asked.reshape(-1), axis=0, mode='clip')  10.3 us
    all_to_all x2, starting transfers between devices, exchange(): return lax.all_to_all(x, 'ex', split_axis=0, concat_axis=0, tiled=True)  7.75 us
    pallas_call x2, Pallas kernels, keep(): call(keep_body, (own, own, pair) * 2, 6, in_specs=[smem] + [vmem] * 4, ou...  5.61 us
    pallas_call x1, Pallas kernels, layer(): call(d_active_body, (shape((rows_e, ff), BF),) * exp_here + (turned,) * e...  5.56 us
  transfers between devices with their start and end apart: 12, of which 9 were waited for; matrix products, arithmetic and copies ran while one was open for 0% of the time, Pallas kernels for 11%

commit v1 on v0

--- a/solution.py
+++ b/solution.py
@@ -130,16 +130,15 @@
     slot0 = rows[2:3, :].astype(I32)
     slot1 = rows[3:4, :].astype(I32)
     per = 4
-    copies = []
+    emb_s[...] = embedded.astype(BF)
+    copies = [pltpu.make_async_copy(emb_s, emb_ref, sems.at[blocks // per])]
+    copies[0].start()
     for n, i in enumerate(range(0, blocks, per)):
         at = lax.broadcasted_iota(I32, (per * routed, tok), 0) + i * routed
         sent = dot(ones_where(jnp.logical_or(at == slot0, at == slot1)), normed).astype(BF)
         out_s[i : i + per] = sent.reshape(per, routed, width)
         copies.append(pltpu.make_async_copy(out_s.at[pl.ds(i, per)], out_ref.at[pl.ds(i, per)], sems.at[n]))
         copies[-1].start()
-    emb_s[...] = embedded.astype(BF)
-    copies.append(pltpu.make_async_copy(emb_s, emb_ref, sems.at[blocks // per]))
-    copies[-1].start()
     for c in copies:
         c.wait()
 
@@ -149,44 +148,83 @@
     return ref[:, j * CAP : (j + 1) * CAP, :].reshape(src * CAP, width)
 
 
-def d_active_body(cot_ref, wd_ref, *outs):
-    for j in range(wd_ref.shape[0]):
+def columns(pre_ref, w_ref, j, into, sems, first):
+    return [
+        pltpu.make_async_copy(
+            w_ref.at[j, :, pl.ds(pl.multiple_of(pre_ref[p] * 128, 128), 128)],
+            into.at[:, pl.ds(p * 128, 128)],
+            sems.at[first + p],
+        )
+        for p in range(8)
+    ]
+
+
+def d_active_body(pre_ref, cot_ref, wd_ref, *refs):
+    outs, (wds, sems) = refs[:4], refs[4:]
+    experts = wd_ref.shape[0]
+    loads = [columns(pre_ref, wd_ref, j, wds.at[j], sems, 8 * j) for j in range(experts)]
+    for group in loads:
+        for c in group:
+            c.start()
+    for j in range(experts):
         cot = expert_rows(cot_ref, j)
-        outs[j][...] = dot(cot, wd_ref[j]).astype(BF)
         outs[2 + j][...] = cot.T
-
-
-def forward_body(j, *refs):
-    x_ref, wg_ref, wu_ref, wd_ref, da_ref = refs[:5]
-    out_ref, mid, xt, wg, wu, wd, das, outs, sin, sout = refs[-10:]
+        for c in loads[j]:
+            c.wait()
+        outs[j][...] = dot(cot, wds[j]).astype(BF)
+
+
+def expert_body(j, *refs):
+    out_s, mid, sin, sout = refs[-4:]
+    if j == 0:
+        pre_ref, x_ref, wg_ref, wu_ref, wd_ref, da_ref, ct_ref, da_next, ct_next = refs[:9]
+        out_ref, keep_ref, xt_ref, sent_ref = refs[9:13]
+        nexts = refs[13:18]
+        wg, wu, wd, das, cts = refs[18:23]
+
+        def loads_of(e, da, ct, into, base):
+            return (
+                columns(pre_ref, wg_ref, e, into[0], sin, base),
+                columns(pre_ref, wu_ref, e, into[1], sin, base + 8),
+                columns(pre_ref, wd_ref, e, into[2], sin, base + 16),
+                [pltpu.make_async_copy(da, into[3], sin.at[base + 24])],
+                [pltpu.make_async_copy(ct, into[4], sin.at[base + 25])],
+            )
+
+        mine = loads_of(0, da_ref, ct_ref, (wg, wu, wd, das, cts), 0)
+        later = loads_of(1, da_next, ct_next, nexts, 26)
+    else:
+        x_ref, wg, wu, wd, das, cts = refs[:6]
+        out_ref, keep_ref, xt_ref, sent_ref = refs[7:11]
+        mine, later = ((),) * 5, ()
+    gates, ups, downs, das_in, cts_in = mine
+    outs = out_s
     _, _, width = outs.shape
-    rows = das.shape[0]
-    loads = [
-        pltpu.make_async_copy(a, b, sin.at[n])
-        for n, (a, b) in enumerate(
-            ((wg_ref.at[j], wg), (wu_ref.at[j], wu), (wd_ref.at[j], wd), (da_ref, das))
-        )
-    ]
-    for c in loads:
-        c.start()
+    rows, ff = das.shape
+    half = ff // 2
+    for group in mine:
+        for c in group:
+            c.start()
+
+    def arrive(group, now=True):
+        if now:
+            for c in group:
+                c.wait()
+
     step = 192
     per = step // CAP
     stores = []
     x = expert_rows(x_ref, j)
-    xt[...] = x.T
     for i in range(rows // step):
         r = slice(i * step, (i + 1) * step)
-        if i == 0:
-            loads[0].wait()
+        arrive(gates, i == 0)
         gate = dot(x[r], wg[...])
-        if i == 0:
-            loads[1].wait()
+        arrive(ups, i == 0)
         up = dot(x[r], wu[...])
         sigmoid = jax.nn.sigmoid(gate)
         silu = gate * sigmoid
         active = (silu * up).astype(BF)
-        if i == 0:
-            loads[2].wait()
+        arrive(downs, i == 0)
         out = dot(active, wd[...], ((1,), (1,))).astype(BF)
         outs[i * per : (i + 1) * per] = out.reshape(per, CAP, width)
         here = pl.ds(i * per, per)
@@ -194,60 +232,56 @@
             pltpu.make_async_copy(outs.at[here], out_ref.at[here, pl.ds(j * CAP, CAP)], sout.at[i])
         )
         stores[-1].start()
-        if i == 0:
-            loads[3].wait()
+        arrive(das_in, i == 0)
         da = das[r].astype(F32)
         d_gate = (da * up * sigmoid * (1.0 + gate * (1.0 - sigmoid))).astype(BF)
         d_up = (da * silu).astype(BF)
-        for g in range(8):
-            c = slice(g * 128, (g + 1) * 128)
-            mid[0, g, r, :] = active[:, c]
-            mid[1, g, r, :] = d_gate[:, c]
-            mid[2, g, r, :] = d_up[:, c]
+        for part, value in enumerate((active, d_gate, d_up)):
+            keep_ref[part, r] = value[:, :half]
+            mid[part, r] = value[:, half:]
+        if i == 0:
+            xt_ref[...] = x.T
+            for group in later:
+                for c in group:
+                    c.start()
+    arrive(cts_in)
+    for part in range(3):
+        got = dot((cts if part == 0 else xt_ref)[...], mid[part]).astype(BF)
+        for i in range(4):
+            sent_ref[part, i] = got[:, i * 128 : (i + 1) * 128]
     for c in stores:
         c.wait()
-
-
-def products(pre_ref, first, ct_ref, xt_ref, mid_ref):
+    for group in later:
+        arrive(group)
+
+
+def keep_body(ct_ref, xt_ref, mid_ref, got_ref, *refs):
+    asend, bsend = refs[2], refs[5]
+    own = refs[6:10]
+    sems = refs[10]
+    ao, an, bo, bn = own
+    there = (refs[0], refs[1], refs[3], refs[4])
+    stores = []
     for part in range(3):
-        lt = (ct_ref if part == 0 else xt_ref)[...]
-        for i in (0, 2):
-            pair = jnp.concatenate(
-                [mid_ref[part, pre_ref[first + i]], mid_ref[part, pre_ref[first + i + 1]]], axis=1
+        got = dot((ct_ref if part == 0 else xt_ref)[...], mid_ref[part])
+        half = got.shape[0] // 2
+        for i in range(4):
+            block = got[:, i * 128 : (i + 1) * 128]
+            total = (block + got_ref[part, i].astype(F32)).astype(BF)
+            a, b = total[:half], total[half:]
+            if i == 0:
+                ao[part], bo[part] = a, b
+            elif i == 1:
+                asend[part, 0], bn[part] = a, b
+            elif i == 2:
+                asend[part, 1], bsend[part, 1] = a, b
+            else:
+                an[part], bsend[part, 0] = a, b
+        for n in range(4):
+            stores.append(
+                pltpu.make_async_copy(own[n].at[part], there[n].at[part], sems.at[4 * part + n])
             )
-            got = dot(lt, pair)
-            yield part, i, got[:, :128]
-            yield part, i + 1, got[:, 128:]
-
-
-def send_body(pre_ref, ct_ref, xt_ref, mid_ref, out_ref):
-    for part, i, block in products(pre_ref, 4, ct_ref, xt_ref, mid_ref):
-        out_ref[part, i] = block.astype(BF)
-
-
-def keep_body(
-    pre_ref, ct_ref, xt_ref, mid_ref, got_ref, *refs
-):
-    asend, bsend = refs[2], refs[5]
-    ao, an, bo, bn, sems = refs[6:]
-    stores = [
-        pltpu.make_async_copy(a, b, sems.at[n])
-        for n, (a, b) in enumerate(zip((ao, an, bo, bn), (refs[0], refs[1], refs[3], refs[4])))
-    ]
-    for part, i, block in products(pre_ref, 0, ct_ref, xt_ref, mid_ref):
-        total = (block + got_ref[part, i].astype(F32)).astype(BF)
-        half = total.shape[0] // 2
-        a, b = total[:half], total[half:]
-        if i == 0:
-            ao[part], bo[part] = a, b
-        elif i == 1:
-            asend[part, 0], bn[part] = a, b
-        elif i == 2:
-            asend[part, 1], bsend[part, 1] = a, b
-        else:
-            an[part], bsend[part, 0] = a, b
-    for c in stores:
-        c.start()
+            stores[-1].start()
     for c in stores:
         c.wait()
 
@@ -298,6 +332,9 @@
     hbm = pl.BlockSpec(memory_space=pltpu.HBM)
     dma = pltpu.SemaphoreType.DMA
 
+    me = lax.axis_index("grp")
+    place = jnp.arange(8, dtype=I32)
+    pre = jnp.bitwise_xor(me // 2, place % 4) * 2 + jnp.bitwise_xor(me % 2, place // 4)
     outbound, rows, cols = call(
         index_body,
         (
@@ -332,63 +369,61 @@
         d_active_body,
         (shape((rows_e, ff), BF),) * exp_here + (turned,) * exp_here,
         56,
-        in_specs=[vmem] * 2,
+        in_specs=[smem, vmem, hbm],
         out_specs=(vmem,) * (2 * exp_here),
-    )(*stay(inbound, w_down))
-
-    me = lax.axis_index("grp")
-    place = jnp.arange(8, dtype=I32)
-    pre = jnp.bitwise_xor(me // 2, place % 4) * 2 + jnp.bitwise_xor(me % 2, place // 4)
+        scratch_shapes=[pltpu.VMEM((exp_here, width, ff), BF), dma((8 * exp_here,))],
+    )(pre, *stay(inbound, w_down))
     core = [(g, g ^ 1) for g in range(8)]
     near1 = [(g, g ^ 2) for g in range(8)]
     near3 = [(g, g ^ 6) for g in range(8)]
-
-    def forward(j, back):
-        return call(
-            lambda *refs: forward_body(j, *refs),
-            (
-                pltpu.HBM((ex_count, routed, width), BF),
-                shape((3, 8, rows_e, 128), BF),
-                turned,
-            ),
-            14,
-            in_specs=[vmem] + [hbm] * (4 + len(back)),
-            out_specs=(hbm, vmem, vmem),
-            input_output_aliases={5: 0} if back else {},
-            scratch_shapes=[
-                pltpu.VMEM((width, ff), BF),
-                pltpu.VMEM((width, ff), BF),
-                pltpu.VMEM((width, ff), BF),
-                pltpu.VMEM((rows_e, ff), BF),
-                pltpu.VMEM((ex_count, CAP, width), BF),
-                dma((4,)),
-                dma((4,)),
-            ],
-        )(in_rows, *stay(w_gate, w_up, w_down, d_active[j], *back))
-
-    def send(j, pre, mid, xt):
-        sent = call(
-            send_body,
-            shape((3, 4, width, 128), BF),
-            6,
-            in_specs=[smem] + [vmem] * 3,
-            out_specs=vmem,
-        )(pre, (ct0, ct1)[j], xt, mid)
-        return sent, lax.ppermute(sent, "grp", core)
+    outs = (
+        pltpu.HBM((ex_count, routed, width), BF),
+        shape((3, rows_e, ff // 2), BF),
+        turned,
+        shape((3, 4, width, 128), BF),
+    )
+    fed = [(width, ff), (width, ff), (width, ff), (rows_e, ff), (width, rows_e)]
+    work = [
+        pltpu.VMEM((ex_count, CAP, width), BF),
+        pltpu.VMEM((3, rows_e, ff // 2), BF),
+    ]
+
+    def expert0():
+        out, mid, xt, sent, *nexts = call(
+            lambda *refs: expert_body(0, *refs),
+            outs + tuple(shape(d, BF) for d in fed),
+            18,
+            in_specs=[smem, vmem] + [hbm] * 7,
+            out_specs=(hbm,) + (vmem,) * 8,
+            scratch_shapes=[pltpu.VMEM(d, BF) for d in fed] + work + [dma((52,)), dma((4,))],
+        )(pre, in_rows, *stay(w_gate, w_up, w_down, d_active[0], ct0, d_active[1], ct1))
+        return out, mid, xt, sent, lax.ppermute(sent, "grp", core), nexts
+
+    def expert1(back, nexts):
+        out, mid, xt, sent = call(
+            lambda *refs: expert_body(1, *refs),
+            outs,
+            12,
+            in_specs=[vmem] * 6 + [hbm],
+            out_specs=(hbm,) + (vmem,) * 3,
+            input_output_aliases={6: 0},
+            scratch_shapes=work + [dma((1,)), dma((4,))],
+        )(in_rows, *nexts, *stay(back))
+        return out, mid, xt, sent, lax.ppermute(sent, "grp", core)
 
     piece = shape((3, width // 2, 128), BF)
     own = pltpu.HBM((3, width // 2, 128), BF)
     pair = shape((3, 2, width // 2, 128), BF)
 
-    def keep(j, pre, mid, xt, crossed):
+    def keep(j, mid, xt, crossed):
         ao, an, asend, bo, bn, bsend = call(
             keep_body,
             (own, own, pair) * 2,
             6,
-            in_specs=[smem] + [vmem] * 4,
+            in_specs=[vmem] * 4,
             out_specs=(hbm, hbm, vmem) * 2,
-            scratch_shapes=[pltpu.VMEM((3, width // 2, 128), BF)] * 4 + [dma((4,))],
-        )(pre, (ct0, ct1)[j], xt, mid, crossed)
+            scratch_shapes=[pltpu.VMEM((3, width // 2, 128), BF)] * 4 + [dma((12,))],
+        )((ct0, ct1)[j], xt, mid, crossed)
         ar = lax.ppermute(asend, "grp", near1)
         br = lax.ppermute(bsend, "grp", near3)
         return ao, an, ar, bo, bn, br
@@ -396,7 +431,7 @@
     def add(ao, an, ar, bo, bn, br):
         snd_a, snd_b = call(
             add_body, (piece,) * 2, 6, in_specs=[vmem] * 4, out_specs=(vmem,) * 2
-        )(an, ar, bn, br)
+        )(*stay(an), ar, *stay(bn), br)
         a_last = lax.ppermute(snd_a, "grp", near3)
         b_last = lax.ppermute(snd_b, "grp", near1)
         return ao, ar, a_last, bo, br, b_last
@@ -413,15 +448,14 @@
         )(*pieces, *grads)
 
     bar = lax.optimization_barrier
-    back, mid0, xt0 = forward(0, ())
-    sent0, crossed0 = send(0, pre, mid0, xt0)
+    back, mid0, xt0, sent0, crossed0, nexts = expert0()
     back, _ = bar((back, sent0))
-    back, mid1, xt1 = forward(1, (back,))
-    sent1, crossed1 = send(1, pre, mid1, xt1)
-    pre0, _ = bar((pre, sent1))
-    kept0 = keep(0, pre0, mid0, xt0, crossed0)
-    pre1, _ = bar((pre, kept0[0]))
-    kept1 = keep(1, pre1, mid1, xt1, crossed1)
+    back, mid1, xt1, sent1, crossed1 = expert1(back, nexts)
+    ct1 = nexts[4]
+    mid0, _ = bar((mid0, sent1))
+    kept0 = keep(0, mid0, xt0, crossed0)
+    xt1, _ = bar((xt1, kept0[0]))
+    kept1 = keep(1, mid1, xt1, crossed1)
     back, _ = bar((back, kept1[0]))
     returned = exchange(back)
     grads = final(0, add(*kept0), ())

time: 172 us -> 169 us (0.983)
  waiting for transfers between devices: 37 us -> 35.2 us
    pallas_call x6 -> x4, Pallas kernels: 23.2 us -> 19.3 us  [the longest x1 9.69 us: expert0(): call(lambda *refs: expert_body(0, *refs), outs + tuple((shape(d, BF) for...]
    pallas_call x2, Pallas kernels: 0.19 us -> 2.28 us  [add(): call(add_body, (piece,) * 2, 6, in_specs=[vmem] * 4, out_specs=(vmem,) * 2)]
  transfers between devices with their start and end apart: 12 -> 12, of which waited for: 9 -> 8; matrix products, arithmetic and copies ran while one was open for 0% -> 0% of each run, Pallas kernels for 11% -> 11%
where the time goes in v1:
time: 169 us
  blocking collectives  63.1 us (37%)
  Pallas kernels  39.7 us (23%)
  waiting for transfers between devices  35.2 us (21%)
  starting transfers between devices  17.8 us (11%)
  local copies, waits for them, and re-layouts  11.6 us (7%)
    all_to_all x2, blocking collectives, exchange(): return lax.all_to_all(x, 'ex', split_axis=0, concat_axis=0, tiled=True)  63.1 us
    all_to_all x2, waiting for transfers between devices, exchange(): return lax.all_to_all(x, 'ex', split_axis=0, concat_axis=0, tiled=True)  14.6 us
    gather x1, local copies, waits for them, and re-layouts, layer(): picked = jnp.take(table, asked.reshape(-1), axis=0, mode='clip')  10.3 us
    pallas_call x1, Pallas kernels, expert0(): call(lambda *refs: expert_body(0, *refs), outs + tuple((shape(d, BF) for...  9.69 us
    ppermute x2, waiting for transfers between devices, keep(): ar = lax.ppermute(asend, 'grp', near1)  9.47 us
    all_to_all x2, starting transfers between devices, exchange(): return lax.all_to_all(x, 'ex', split_axis=0, concat_axis=0, tiled=True)  7.62 us
    pallas_call x1, Pallas kernels, layer(): call(d_active_body, (shape((rows_e, ff), BF),) * exp_here + (turned,) * e...  6.35 us
    ppermute x2, waiting for transfers between devices, keep(): br = lax.ppermute(bsend, 'grp', near3)  5.48 us
  transfers between devices with their start and end apart: 12, of which 8 were waited for; matrix products, arithmetic and copies ran while one was open for 0% of the time, Pallas kernels for 11%

profile of v1, /device:TPU:0, one launch (start us, length us, event | category | flops | bytes accessed | tf_op | source)
XLA Modules:
  0.0 168.8 jit_solution(8776179708565671654)
XLA Ops:
  0.6 4.1 %shard_map.129 = (bf16[16,104,512]{2,1,0:T(8,128)(2,1)}, f32[8,512]{1,0:T(8,128)}, f32[512,8]{1,0:T(8,128)}) custom-call(s32[2]{0:T(128)} %len_ref.1, s32[2,256]{1,0:T(2,128)} %ids_ref.1, s32[2,512]{1,0:T(2,128)} %bitcast.14, f32[2,512]{1,0:T(2,128)} %bitcast.15, bf16[512,512]{1,0:T(8,128)(2,1)} %d_ref.1), custom_call_target="tpu_custom_call" | custom-call | tf_op jit(solution)/shard_map/pallas_call | solution.py:338
  4.8 32.3 %all_to_all.20.cot_ref = bf16[16,104,512]{2,1,0:T(8,128)(2,1)S(1)} all-to-all(bf16[16,104,512]{2,1,0:T(8,128)(2,1)} %get-tuple-element.54), channel_id=1, replica_groups=mesh['grp'=8,'ex'=16] {'ex'}, dimensions={0} | all-to-all | bytes 3407872 | tf_op jit(solution)/shard_map/all_to_all | solution.py:317
  37.1 1.2 copy-done.10
  38.3 10.3 %gather_fusion = bf16[2048,512]{1,0:T(8,128)(2,1)S(1)} fusion(bf16[4096,512]{1,0:T(8,128)(2,1)} %param.14, s32[2048]{0:T(1024)S(1)} %fusion.2), kind=kCustom, calls=%fused_computation | custom fusion | bytes 4202496 | tf_op jit(solution)/shard_map/jit(_take)/gather | solution.py:352
  48.7 30.8 %all_to_all.21.got_ref = bf16[16,128,512]{2,1,0:T(8,128)(2,1)S(1)} all-to-all(bf16[16,128,512]{2,1,0:T(8,128)(2,1)S(1)} %bitcast.12), channel_id=1, replica_groups=mesh['grp'=8,'ex'=16] {'ex'}, dimensions={0} | all-to-all | bytes 4194304 | tf_op jit(solution)/shard_map/all_to_all | solution.py:317
  79.5 3.2 %shard_map.130 = (bf16[512,512]{1,0:T(8,128)(2,1)}, bf16[16,96,512]{2,1,0:T(8,128)(2,1)}) custom-call(f32[8,512]{1,0:T(8,128)S(1)} %copy-done.7, f32[512,8]{1,0:T(8,128)S(1)} %copy-done.1, f32[1,512]{1,0:T(1,128)S(1)} %bitcast.11, bf16[16,128,512]{2,1,0:T(8,128)(2,1)S(1)} %all_to_all.21.got_ref), custom_call_target="tpu_custom_call" | custom-call | tf_op jit(solution)/shard_map/pallas_call | solution.py:354
  82.7 3.9 %all-to-all-start.2 = ((bf16[16,96,512]{2,1,0:T(8,128)(2,1)}), bf16[16,96,512]{2,1,0:T(8,128)(2,1)S(1)}, u32[]{:S(2)}, u32[]{:S(2)}) async-start(bf16[16,96,512]{2,1,0:T(8,128)(2,1)} %get-tuple-element.56), calls=%async_computation.2 | async-start | bytes 3145728 | tf_op jit(solution)/shard_map/all_to_all | solution.py:317
  87.1 6.3 %shard_map.131 = (bf16[768,1024]{1,0:T(8,128)(2,1)}, bf16[768,1024]{1,0:T(8,128)(2,1)}, bf16[512,768]{1,0:T(8,128)(2,1)}, bf16[512,768]{1,0:T(8,128)(2,1)}) custom-call(s32[8]{0:T(128)} %fusion.5.pre_ref.refs_0_, bf16[16,104,512]{2,1,0:T(8,128)(2,1)} %copy-done.10, bf16[2,512,1024]{2,1,0:T(8,128)(2,1)} %refs_4_.1), custom_call_target="tpu_custom_call" | custom-call | tf_op jit(solution)/shard_map/pallas_call | solution.py:368
  93.5 14.6 %all-to-all-done.2.refs_1_.refs_0_ = bf16[16,96,512]{2,1,0:T(8,128)(2,1)S(1)} async-done(((bf16[16,96,512]{2,1,0:T(8,128)(2,1)}), bf16[16,96,512]{2,1,0:T(8,128)(2,1)S(1)}, u32[]{:S(2)}, u32[]{:S(2)}) %all-to-all-start.2) | async-done | bytes 1572896 | tf_op jit(solution)/shard_map/all_to_all | solution.py:317
  108.1 9.7 %shard_map.132 = (bf16[16,96,512]{2,1,0:T(8,128)(2,1)}, bf16[3,768,512]{2,1,0:T(8,128)(2,1)S(1)}, bf16[512,768]{1,0:T(8,128)(2,1)S(1)}, bf16[3,4,512,128]{3,2,1,...) custom-call(s32[8]{0:T(128)S(1)} %copy-done.8, ...), custom_call_target="tpu_custom_call" | custom-call | tf_op jit(solution)/shard_map/pallas_call | solution.py:392
  117.9 5.3 %shard_map.133 = (bf16[16,96,512]{2,1,0:T(8,128)(2,1)}, bf16[3,768,512]{2,1,0:T(8,128)(2,1)S(1)}, bf16[512,768]{1,0:T(8,128)(2,1)S(1)}, bf16[3,4,512,128]{3,2,1,0:T(8,128)(2,1)S(1)}) custom-call(bf16[16,96,512]{2,1,0:T(8,128)(2,1)S(1)} %all-to-all-done.2.refs_1_.refs_0_, ...), custom_call_target="tpu_custom_call", output_to_operand_aliasing={{0}: (6, {})} | custom-call | tf_op jit(solution)/shard_map/pallas_call | solution.py:403
  123.2 0.8 collective-permute-start.1
  124.0 2.1 %shard_map.134 = (bf16[3,256,128]{2,1,0:T(8,128)(2,1)}, bf16[3,256,128]{2,1,0:T(8,128)(2,1)}, bf16[3,2,256,128]{3,2,1,0:T(8,128)(2,1)S(1)}, bf16[3,256,128]{2,1,...) custom-call(bf16[512,768]{1,0:T(8,128)(2,1)S(1)} %copy-done, ...), custom_call_target="tpu_custom_call" | custom-call | tf_op jit(solution)/shard_map/pallas_call | solution.py:419
  126.2 0.9 collective-permute-done.1.got_ref
  127.1 2.1 %shard_map.135 = (bf16[3,256,128]{2,1,0:T(8,128)(2,1)}, bf16[3,256,128]{2,1,0:T(8,128)(2,1)}, bf16[3,2,256,128]{3,2,1,0:T(8,128)(2,1)S(1)}, bf16[3,256,128]{2,1,...) custom-call(bf16[512,768]{1,0:T(8,128)(2,1)S(1)} %get-tuple-element.65.refs_5_.ct_ref, ...), custom_call_target="tpu_custom_call" | custom-call | tf_op jit(solution)/shard_map/pallas_call | solution.py:419
  129.2 3.7 %all-to-all-start.3 = ((bf16[16,96,512]{2,1,0:T(8,128)(2,1)}), bf16[16,96,512]{2,1,0:T(8,128)(2,1)S(1)}, u32[]{:S(2)}, u32[]{:S(2)}) async-start(bf16[16,96,512]{2,1,0:T(8,128)(2,1)} %get-tuple-element.79), calls=%async_computation.3 | async-start | bytes 3145728 | tf_op jit(solution)/shard_map/all_to_all | solution.py:317
  133.0 1.6 collective-permute-start.6
  134.6 2.1 %collective-permute-start.7 = (bf16[3,2,256,128]{3,2,1,0:T(8,128)(2,1)S(1)}, bf16[3,2,256,128]{3,2,1,0:T(8,128)(2,1)S(1)}, u32[]{:S(2)}, u32[]{:S(2)}) collective-permute-start(bf16[3,2,256,128]{3,2,1,0:T(8,128)(2,1)S(1)} %get-tuple-element.90), channel_id=1, source_target_pairs={{0,96},{16,112},{32,64},{48,80},{64,32},{80,48},{96,0},{112,16},{1... | collective-permute-start | bytes 1179656 | tf_op jit(solution)/shard_map/ppermute | solution.py:428
  136.7 0.6 collective-permute-start.2
  137.9 7.1 %collective-permute-done.6.ar.refs_1_ = bf16[3,2,256,128]{3,2,1,0:T(8,128)(2,1)S(1)} collective-permute-done((bf16[3,2,256,128]{3,2,1,0:T(8,128)(2,1)S(1)}, bf16[3,2,256,128]{3,2,1,0:T(8,128)(2,1)S(1)}, u32[]{:S(2)}, u32[]{:S(2)}) %collective-permute-start.6) | collective-permute-done | bytes 393248 | tf_op jit(solution)/shard_map/ppermute | solution.py:427
  145.0 2.7 %collective-permute-done.7.br.refs_4_ = bf16[3,2,256,128]{3,2,1,0:T(8,128)(2,1)S(1)} collective-permute-done((bf16[3,2,256,128]{3,2,1,0:T(8,128)(2,1)S(1)}, bf16[3,2,256,128]{3,2,1,0:T(8,128)(2,1)S(1)}, u32[]{:S(2)}, u32[]{:S(2)}) %collective-permute-start.7) | collective-permute-done | bytes 393248 | tf_op jit(solution)/shard_map/ppermute | solution.py:428
  147.8 1.2 shard_map.138
  148.9 2.2 %collective-permute-start.8 = (bf16[3,256,128]{2,1,0:T(8,128)(2,1)S(1)}, bf16[3,256,128]{2,1,0:T(8,128)(2,1)S(1)}, u32[]{:S(2)}, u32[]{:S(2)}) collective-permute-start(bf16[3,256,128]{2,1,0:T(8,128)(2,1)S(1)} %get-tuple-element.91), channel_id=1, source_target_pairs={{0,96},{16,112},{32,64},{48,80},{64,32},{80,48},{96,0},{112,16},{1... | collective-permute-start | bytes 589832 | tf_op jit(solution)/shard_map/ppermute | solution.py:435
  151.1 2.3 %collective-permute-done.2.ar.refs_1_ = bf16[3,2,256,128]{3,2,1,0:T(8,128)(2,1)S(1)} collective-permute-done((bf16[3,2,256,128]{3,2,1,0:T(8,128)(2,1)S(1)}, bf16[3,2,256,128]{3,2,1,0:T(8,128)(2,1)S(1)}, u32[]{:S(2)}, u32[]{:S(2)}) %collective-permute-start.2) | collective-permute-done | bytes 393248 | tf_op jit(solution)/shard_map/ppermute | solution.py:427
  153.5 2.7 %collective-permute-done.3.br.refs_4_ = bf16[3,2,256,128]{3,2,1,0:T(8,128)(2,1)S(1)} collective-permute-done((bf16[3,2,256,128]{3,2,1,0:T(8,128)(2,1)S(1)}, bf16[3,2,256,128]{3,2,1,0:T(8,128)(2,1)S(1)}, u32[]{:S(2)}, u32[]{:S(2)}) %collective-permute-start.3) | collective-permute-done | bytes 393248 | tf_op jit(solution)/shard_map/ppermute | solution.py:428
  156.2 1.1 shard_map.137
  157.3 2.2 %collective-permute-start.4 = (bf16[3,256,128]{2,1,0:T(8,128)(2,1)S(1)}, bf16[3,256,128]{2,1,0:T(8,128)(2,1)S(1)}, u32[]{:S(2)}, u32[]{:S(2)}) collective-permute-start(bf16[3,256,128]{2,1,0:T(8,128)(2,1)S(1)} %get-tuple-element.84), channel_id=1, source_target_pairs={{0,96},{16,112},{32,64},{48,80},{64,32},{80,48},{96,0},{112,16},{1... | collective-permute-start | bytes 589832 | tf_op jit(solution)/shard_map/ppermute | solution.py:435
  159.5 0.9 shard_map.139
  160.5 3.8 %collective-permute-done.4.refs_2_ = bf16[3,256,128]{2,1,0:T(8,128)(2,1)S(1)} collective-permute-done((bf16[3,256,128]{2,1,0:T(8,128)(2,1)S(1)}, bf16[3,256,128]{2,1,0:T(8,128)(2,1)S(1)}, u32[]{:S(2)}, u32[]{:S(2)}) %collective-permute-start.4) | collective-permute-done | bytes 196640 | tf_op jit(solution)/shard_map/ppermute | solution.py:435
  164.3 0.9 collective-permute-done.5.refs_5_
  165.2 0.9 shard_map.140
  166.1 2.7 %shard_map.136 = bf16[512,512]{1,0:T(8,128)(2,1)} custom-call(f32[512,8]{1,0:T(8,128)S(1)} %copy-done.1, bf16[512,512]{1,0:T(8,128)(2,1)S(1)} %copy-done.2, bf16[16,96,512]{2,1,0:T(8,128)(2,1)S(1)} %all-to-all-done.3.ret_ref), custom_call_target="tpu_custom_call" | custom-call | tf_op jit(solution)/shard_map/pallas_call | solution.py:463
  (33 shorter events, 1.3 us)
Async XLA Ops:
  37.1 1.2 copy-start.10
  48.7 30.8 %copy-start.1 = (f32[512,8]{1,0:T(8,128)S(1)}, f32[512,8]{1,0:T(8,128)}, u32[]{:S(2)}) copy-start(f32[512,8]{1,0:T(8,128)} %get-tuple-element.52.cols_ref) | copy-start | bytes 49156
  48.7 30.8 %copy-start.7 = (f32[8,512]{1,0:T(8,128)S(1)}, f32[8,512]{1,0:T(8,128)}, u32[]{:S(2)}) copy-start(f32[8,512]{1,0:T(8,128)} %get-tuple-element.53.rows_ref) | copy-start | bytes 49156
  48.7 30.8 %copy-start.9 = (f32[512]{0:T(512)S(1)}, f32[512]{0:T(512)}, u32[]{:S(2)}) copy-start(f32[512]{0:T(512)} %param.15) | copy-start | bytes 6148
  82.7 25.4 %all-to-all-start.2 = ((bf16[16,96,512]{2,1,0:T(8,128)(2,1)}), bf16[16,96,512]{2,1,0:T(8,128)(2,1)S(1)}, u32[]{:S(2)}, u32[]{:S(2)}) async-start(bf16[16,96,512]{2,1,0:T(8,128)(2,1)} %get-tuple-element.56), calls=%async_computation.2 | async-start | bytes 3145728 | tf_op jit(solution)/shard_map/all_to_all | solution.py:317
  87.1 21.0 %copy-start.8 = (s32[8]{0:T(128)S(1)}, s32[8]{0:T(128)}, u32[]{:S(2)}) copy-start(s32[8]{0:T(128)} %fusion.5.pre_ref.refs_0_) | copy-start | bytes 100
  117.8 6.2 %collective-permute-start = (bf16[3,4,512,128]{3,2,1,0:T(8,128)(2,1)S(1)}, bf16[3,4,512,128]{3,2,1,0:T(8,128)(2,1)S(1)}, u32[]{:S(2)}, u32[]{:S(2)}) collective-permute-start(bf16[3,4,512,128]{3,2,1,0:T(8,128)(2,1)S(1)} %get-tuple-element.67), channel_id=1, source_target_pairs={{0,16},{16,0},{32,48},{48,32},{64,80},{80,64},{96,112},{112,96},{1... | collective-permute-start | bytes 4718600 | tf_op jit(solution)/shard_map/ppermute | solution.py:400
  117.9 6.1 %copy-start = (bf16[512,768]{1,0:T(8,128)(2,1)S(1)}, bf16[512,768]{1,0:T(8,128)(2,1)}, u32[]{:S(2)}) copy-start(bf16[512,768]{1,0:T(8,128)(2,1)} %get-tuple-element.58.refs_6_.ct_ref) | copy-start | bytes 2359300
  123.2 3.8 %collective-permute-start.1 = (bf16[3,4,512,128]{3,2,1,0:T(8,128)(2,1)S(1)}, bf16[3,4,512,128]{3,2,1,0:T(8,128)(2,1)S(1)}, u32[]{:S(2)}, u32[]{:S(2)}) collective-permute-start(bf16[3,4,512,128]{3,2,1,0:T(8,128)(2,1)S(1)} %get-tuple-element.73), channel_id=1, source_target_pairs={{0,16},{16,0},{32,48},{48,32},{64,80},{80,64},{96,112},{112,96},{1... | collective-permute-start | bytes 4718600 | tf_op jit(solution)/shard_map/ppermute | solution.py:412
  129.2 36.9 %all-to-all-start.3 = ((bf16[16,96,512]{2,1,0:T(8,128)(2,1)}), bf16[16,96,512]{2,1,0:T(8,128)(2,1)S(1)}, u32[]{:S(2)}, u32[]{:S(2)}) async-start(bf16[16,96,512]{2,1,0:T(8,128)(2,1)} %get-tuple-element.79), calls=%async_computation.3 | async-start | bytes 3145728 | tf_op jit(solution)/shard_map/all_to_all | solution.py:317
  132.9 26.6 %copy-start.5 = (bf16[3,256,128]{2,1,0:T(8,128)(2,1)S(1)}, bf16[3,256,128]{2,1,0:T(8,128)(2,1)}, u32[]{:S(2)}) copy-start(bf16[3,256,128]{2,1,0:T(8,128)(2,1)} %get-tuple-element.75.refs_0_) | copy-start | bytes 589828
  133.0 26.6 %copy-start.6 = (bf16[3,256,128]{2,1,0:T(8,128)(2,1)S(1)}, bf16[3,256,128]{2,1,0:T(8,128)(2,1)}, u32[]{:S(2)}) copy-start(bf16[3,256,128]{2,1,0:T(8,128)(2,1)} %get-tuple-element.92.refs_3_) | copy-start | bytes 589828
  133.0 12.1 %collective-permute-start.6 = (bf16[3,2,256,128]{3,2,1,0:T(8,128)(2,1)S(1)}, bf16[3,2,256,128]{3,2,1,0:T(8,128)(2,1)S(1)}, u32[]{:S(2)}, u32[]{:S(2)}) collective-permute-start(bf16[3,2,256,128]{3,2,1,0:T(8,128)(2,1)S(1)} %get-tuple-element.87), channel_id=1, source_target_pairs={{0,32},{16,48},{32,0},{48,16},{64,96},{80,112},{96,64},{112,80},{1... | collective-permute-start | bytes 1179656 | tf_op jit(solution)/shard_map/ppermute | solution.py:427
  134.6 13.2 %collective-permute-start.7 = (bf16[3,2,256,128]{3,2,1,0:T(8,128)(2,1)S(1)}, bf16[3,2,256,128]{3,2,1,0:T(8,128)(2,1)S(1)}, u32[]{:S(2)}, u32[]{:S(2)}) collective-permute-start(bf16[3,2,256,128]{3,2,1,0:T(8,128)(2,1)S(1)} %get-tuple-element.90), channel_id=1, source_target_pairs={{0,96},{16,112},{32,64},{48,80},{64,32},{80,48},{96,0},{112,16},{1... | collective-permute-start | bytes 1179656 | tf_op jit(solution)/shard_map/ppermute | solution.py:428
  136.7 16.8 %collective-permute-start.2 = (bf16[3,2,256,128]{3,2,1,0:T(8,128)(2,1)S(1)}, bf16[3,2,256,128]{3,2,1,0:T(8,128)(2,1)S(1)}, u32[]{:S(2)}, u32[]{:S(2)}) collective-permute-start(bf16[3,2,256,128]{3,2,1,0:T(8,128)(2,1)S(1)} %get-tuple-element.80), channel_id=1, source_target_pairs={{0,32},{16,48},{32,0},{48,16},{64,96},{80,112},{96,64},{112,80},{1... | collective-permute-start | bytes 1179656 | tf_op jit(solution)/shard_map/ppermute | solution.py:427
  137.3 18.9 %collective-permute-start.3 = (bf16[3,2,256,128]{3,2,1,0:T(8,128)(2,1)S(1)}, bf16[3,2,256,128]{3,2,1,0:T(8,128)(2,1)S(1)}, u32[]{:S(2)}, u32[]{:S(2)}) collective-permute-start(bf16[3,2,256,128]{3,2,1,0:T(8,128)(2,1)S(1)} %get-tuple-element.83), channel_id=1, source_target_pairs={{0,96},{16,112},{32,64},{48,80},{64,32},{80,48},{96,0},{112,16},{1... | collective-permute-start | bytes 1179656 | tf_op jit(solution)/shard_map/ppermute | solution.py:428
  147.8 17.4 %copy-start.3 = (bf16[3,256,128]{2,1,0:T(8,128)(2,1)S(1)}, bf16[3,256,128]{2,1,0:T(8,128)(2,1)}, u32[]{:S(2)}) copy-start(bf16[3,256,128]{2,1,0:T(8,128)(2,1)} %get-tuple-element.78.refs_0_) | copy-start | bytes 589828
  147.8 17.4 %copy-start.4 = (bf16[3,256,128]{2,1,0:T(8,128)(2,1)S(1)}, bf16[3,256,128]{2,1,0:T(8,128)(2,1)}, u32[]{:S(2)}) copy-start(bf16[3,256,128]{2,1,0:T(8,128)(2,1)} %get-tuple-element.85.refs_3_) | copy-start | bytes 589828
  148.9 10.6 %collective-permute-start.8 = (bf16[3,256,128]{2,1,0:T(8,128)(2,1)S(1)}, bf16[3,256,128]{2,1,0:T(8,128)(2,1)S(1)}, u32[]{:S(2)}, u32[]{:S(2)}) collective-permute-start(bf16[3,256,128]{2,1,0:T(8,128)(2,1)S(1)} %get-tuple-element.91), channel_id=1, source_target_pairs={{0,96},{16,112},{32,64},{48,80},{64,32},{80,48},{96,0},{112,16},{1... | collective-permute-start | bytes 589832 | tf_op jit(solution)/shard_map/ppermute | solution.py:435
  151.1 8.4 %collective-permute-start.9 = (bf16[3,256,128]{2,1,0:T(8,128)(2,1)S(1)}, bf16[3,256,128]{2,1,0:T(8,128)(2,1)S(1)}, u32[]{:S(2)}, u32[]{:S(2)}) collective-permute-start(bf16[3,256,128]{2,1,0:T(8,128)(2,1)S(1)} %get-tuple-element.93), channel_id=1, source_target_pairs={{0,32},{16,48},{32,0},{48,16},{64,96},{80,112},{96,64},{112,80},{1... | collective-permute-start | bytes 589832 | tf_op jit(solution)/shard_map/ppermute | solution.py:436
  157.3 7.0 %collective-permute-start.4 = (bf16[3,256,128]{2,1,0:T(8,128)(2,1)S(1)}, bf16[3,256,128]{2,1,0:T(8,128)(2,1)S(1)}, u32[]{:S(2)}, u32[]{:S(2)}) collective-permute-start(bf16[3,256,128]{2,1,0:T(8,128)(2,1)S(1)} %get-tuple-element.84), channel_id=1, source_target_pairs={{0,96},{16,112},{32,64},{48,80},{64,32},{80,48},{96,0},{112,16},{1... | collective-permute-start | bytes 589832 | tf_op jit(solution)/shard_map/ppermute | solution.py:435
  159.5 5.7 %collective-permute-start.5 = (bf16[3,256,128]{2,1,0:T(8,128)(2,1)S(1)}, bf16[3,256,128]{2,1,0:T(8,128)(2,1)S(1)}, u32[]{:S(2)}, u32[]{:S(2)}) collective-permute-start(bf16[3,256,128]{2,1,0:T(8,128)(2,1)S(1)} %get-tuple-element.86), channel_id=1, source_target_pairs={{0,32},{16,48},{32,0},{48,16},{64,96},{80,112},{96,64},{112,80},{1... | collective-permute-start | bytes 589832 | tf_op jit(solution)/shard_map/ppermute | solution.py:436
  160.5 5.6 %copy-start.2 = (bf16[512,512]{1,0:T(8,128)(2,1)S(1)}, bf16[512,512]{1,0:T(8,128)(2,1)}, u32[]{:S(2)}) copy-start(bf16[512,512]{1,0:T(8,128)(2,1)} %get-tuple-element.55.emb_ref) | copy-start | bytes 1572868
